TPU v7x, 32 devices: a whole 2x2x4 slice. The times are simulated.
32 devices in a mesh: dap: 8 (over z, x), cplx: 4 (over y, core).
Axes of the slice: x: 2, y: 2, z: 4, core: 2. Of those that a mesh axis runs over, the one named last changes fastest.
Arguments:
- pair: bfloat16 [96, 384, 128], P('dap', 'cplx'), parts along dimension 1, may hold values from -6 to 6
- cotangent: bfloat16 [96, 384, 128], P('dap', 'cplx'), parts along dimension 1, may hold values from -6 to 6
- residue_mask: int32 [384], P('cplx'), parts along dimension 0, may hold values 0 or 1
- chain_ids: int32 [384], P('cplx'), parts along dimension 0, may hold values from 0 to 2, never falling along the last dimension, each value on 1 to 48 neighbouring positions
- chain_embed: float32 [2, 128], replicated, may hold values from -4 to 4
- out_norm_gain: float32 [128], replicated, may hold values from 0.25 to 1.75
- out_proj: bfloat16 [128, 512], replicated, may hold values from -0.5 to 0.5
- out_gate: bfloat16 [128, 128], replicated, may hold values from -0.5 to 0.5
- out_mid_gain: float32 [128], replicated, may hold values from 0.25 to 1.75
- out_final: bfloat16 [128, 128], replicated, may hold values from -0.5 to 0.5
- in_norm_gain: float32 [128], replicated, may hold values from 0.25 to 1.75
- in_proj: bfloat16 [128, 512], replicated, may hold values from -0.5 to 0.5
- in_gate: bfloat16 [128, 128], replicated, may hold values from -0.5 to 0.5
- in_mid_gain: float32 [128], replicated, may hold values from 0.25 to 1.75
- in_final: bfloat16 [128, 128], replicated, may hold values from -0.5 to 0.5
Outputs:
- pair_grad: bfloat16 [96, 384, 128], P('dap', 'cplx'), parts along dimension 1
- grad_proj: float32 [512, 512], P('cplx'), parts along dimension 0
- grad_gate: float32 [512, 128], P('cplx'), parts along dimension 0
- grad_final: float32 [512, 128], P('cplx'), parts along dimension 0
- grad_norm_gain: float32 [512], P('cplx'), parts along dimension 0
- grad_mid_gain: float32 [512], P('cplx'), parts along dimension 0
There are 4 independent parts, one for each index of `cplx`. A program takes and returns all parts, laid end to end along the dimension named above; an argument that names none is the same for every part. Nothing has to cross between parts.
Inputs may be any that keep to these rules, and one draw needn't show every extreme that they name: `chain_ids`: chain numbers never fall along the residues; each chain has at most 48 residues.
All inputs are finite; a program needn't handle non-finite values.
Results may differ from a plain program's by a relative error of at most 0.019.
Values may be sent and summed in bfloat16 or wider, within the bound.
A program may use at most 128 MiB of HBM per device.

v0:
```python
import jax
import jax.numpy as jnp
from jax import lax
from jax.sharding import PartitionSpec as P


def layer_norm(values_in, gain):
    average = jnp.mean(values_in, axis=-1, keepdims=True)
    centred = values_in - average
    variance = jnp.mean(centred * centred, axis=-1, keepdims=True)
    return centred * lax.rsqrt(variance + 1e-05) * gain


def gated_pair(projected, pair_mask, hidden_width):
    masked = pair_mask[..., None]
    left_act = (
        masked
        * jax.nn.sigmoid(projected[..., :hidden_width])
        * projected[..., hidden_width : 2 * hidden_width]
    )
    right_act = (
        masked
        * jax.nn.sigmoid(projected[..., 2 * hidden_width : 3 * hidden_width])
        * projected[..., 3 * hidden_width :]
    )
    return (left_act, right_act)


def shards(
    pair,
    cotangent,
    residue_mask,
    chain_ids,
    chain_embed,
    out_norm_gain,
    out_proj,
    out_gate,
    out_mid_gain,
    out_final,
    in_norm_gain,
    in_proj,
    in_gate,
    in_mid_gain,
    in_final,
):
    f32 = jnp.float32
    bf16 = jnp.bfloat16
    row_count = pair.shape[0]
    res_count = pair.shape[1]
    hidden_width = out_final.shape[0]
    inv_count = 1.0 / res_count
    row_start = lax.axis_index("dap") * row_count
    row_mask = lax.dynamic_slice_in_dim(residue_mask, row_start, row_count, 0)
    row_chain = lax.dynamic_slice_in_dim(chain_ids, row_start, row_count, 0)
    pair_mask = (row_mask[:, None] * residue_mask[None, :]).astype(f32)
    same_chain = row_chain[:, None] == chain_ids[None, :]
    start = pair.astype(f32) + jnp.where(same_chain[..., None], chain_embed[1], chain_embed[0])
    out_normed = layer_norm(start, out_norm_gain).astype(bf16)
    projected = jnp.dot(out_normed, out_proj, preferred_element_type=f32)
    left_act, right_act = gated_pair(projected, pair_mask, hidden_width)
    left_b = left_act.astype(bf16)
    right_b = right_act.astype(bf16)
    x_out = jnp.einsum(
        "ikc,jkc->ijc",
        left_b,
        lax.all_gather(right_b, "dap", axis=0, tiled=True),
        preferred_element_type=f32,
    )
    y_out = layer_norm(x_out, out_mid_gain).astype(bf16)
    update = jax.nn.sigmoid(jnp.dot(out_normed, out_gate, preferred_element_type=f32)) * jnp.dot(
        y_out, out_final, preferred_element_type=f32
    )
    pair_mid = (start + update).astype(bf16)
    mid_f32 = pair_mid.astype(f32)
    normed_f32, norm_back = jax.vjp(layer_norm, mid_f32, in_norm_gain)
    in_normed = normed_f32.astype(bf16)
    proj_in = jnp.dot(in_normed, in_proj, preferred_element_type=f32)
    (left_in, right_in), glu_back = jax.vjp(
        lambda proj_val: gated_pair(proj_val, pair_mask, hidden_width), proj_in
    )
    left_ib = left_in.astype(bf16)
    right_ib = right_in.astype(bf16)
    columns = lax.all_to_all(left_ib, "dap", split_axis=1, concat_axis=0, tiled=True)
    left_block = columns
    x_in = jnp.einsum(
        "kic,kjc->ijc",
        left_block,
        lax.all_gather(right_ib, "dap", axis=0, tiled=True),
        preferred_element_type=f32,
    )
    y_f32, mid_back = jax.vjp(layer_norm, x_in, in_mid_gain)
    y_in = y_f32.astype(bf16)
    logit = jnp.dot(in_normed, in_gate, preferred_element_type=f32)
    value = jnp.dot(y_in, in_final, preferred_element_type=f32)
    sigma = jax.nn.sigmoid(logit)
    upstream = cotangent.astype(f32)
    grad_value = (upstream * sigma).astype(bf16)
    grad_logit = (upstream * value * sigma * (1.0 - sigma)).astype(bf16)
    grad_final = jnp.einsum("ijc,ijd->cd", y_in, grad_value, preferred_element_type=f32) * inv_count
    grad_gate = (
        jnp.einsum("ijc,ijd->cd", in_normed, grad_logit, preferred_element_type=f32) * inv_count
    )
    grad_y = jnp.dot(grad_value, in_final.T, preferred_element_type=f32)
    grad_x, grad_mid = mid_back(grad_y)
    grad_x_b = grad_x.astype(bf16)
    shard_rows = lax.all_gather(grad_x_b, "dap", axis=0, tiled=True)
    left_block = left_ib
    grad_right = jnp.einsum("kic,ijc->kjc", left_block, shard_rows, preferred_element_type=f32)
    new_block = jnp.einsum("kjc,ijc->kic", right_ib, shard_rows, preferred_element_type=f32)
    grad_p = glu_back((new_block, grad_right))[0].astype(bf16)
    grad_proj = jnp.einsum("ijc,ijd->cd", in_normed, grad_p, preferred_element_type=f32) * inv_count
    grad_normed = jnp.dot(grad_p, in_proj.T, preferred_element_type=f32) + jnp.dot(
        grad_logit, in_gate.T, preferred_element_type=f32
    )
    grad_z, grad_norm = norm_back(grad_normed)
    pair_grad = (upstream + grad_z).astype(bf16)
    reduced = (
        lax.psum(grad_proj.astype(jnp.bfloat16), "dap").astype(jnp.float32),
        lax.psum(grad_gate.astype(jnp.bfloat16), "dap").astype(jnp.float32),
        lax.psum(grad_final.astype(jnp.bfloat16), "dap").astype(jnp.float32),
        lax.psum((grad_norm * inv_count).astype(jnp.bfloat16), "dap").astype(jnp.float32),
        lax.psum((grad_mid * inv_count).astype(jnp.bfloat16), "dap").astype(jnp.float32),
    )
    return (pair_grad, reduced[0], reduced[1], reduced[2], reduced[3], reduced[4])


def solution(mesh):
    placed = (
        P("dap", "cplx", None),
        P("dap", "cplx", None),
        P("cplx"),
        P("cplx"),
        P(),
        P(),
        P(),
        P(),
        P(),
        P(),
        P(),
        P(),
        P(),
        P(),
        P(),
    )
    return jax.shard_map(
        shards,
        mesh=mesh,
        in_specs=placed,
        out_specs=(
            P("dap", "cplx", None),
            P("cplx", None),
            P("cplx", None),
            P("cplx", None),
            P("cplx"),
            P("cplx"),
        ),
        check_vma=False,
    )
```

profile of v0, /device:TPU:0, one launch (start us, length us, event | category | flops | bytes accessed | tf_op | source)
XLA Modules:
  0.0 371.3 jit_solution(1143531026395006253)
XLA Ops:
  7.2 0.7 dynamic_slice.7
  8.0 0.7 broadcast_compare_fusion
  8.7 0.8 slice_bitcast_fusion.1
  9.5 1.4 fusion.41
  10.9 1.6 multiply_reduce_fusion.7
  12.5 0.7 dynamic_slice.6
  13.2 0.7 multiply_convert_fusion.10
  13.9 1.9 fusion.47
  15.9 1.1 fusion.28
  17.0 1.2 copy.47
  18.3 1.7 fusion.8
  19.9 51.8 %all-gather.4.cloned.1.call-done = bf16[96,96,128]{2,1,0:T(8,128)(2,1)} async-done(((bf16[12,96,128]{2,1,0:T(8,128)(2,1)}), bf16[96,96,128]{2,1,0:T(8,128)(2,1)}) %all-gather.4.cloned.1.call-update) | async-done | bytes 2359312 | tf_op jit(solution)/shard_map/all_gather | solution.py:66
  71.7 3.5 copy.46
  75.2 2.8 fusion.62
  78.5 0.5 copy-done.6
  79.2 0.6 fusion.63
  79.9 0.5 multiply_reduce_fusion.6
  80.3 0.3 copy-done.2
  80.7 0.4 multiply_convert_fusion.4
  81.1 0.4 fusion.45
  81.5 1.4 copy-done.1
  82.9 1.1 multiply_convert_fusion.2
  84.0 0.9 copy.49
  84.9 3.5 all-to-all-start
  88.4 1.1 fusion.5
  89.5 17.3 %all-to-all-done = bf16[12,96,128]{2,0,1:T(8,128)(2,1)S(1)} async-done(((bf16[12,96,128]{2,0,1:T(8,128)(2,1)}), bf16[12,96,128]{2,0,1:T(8,128)(2,1)S(1)}, u32[]{:S(2)}, u32[]{:S(2)}) %all-to-all-start) | async-done | bytes 294944 | tf_op jit(solution)/shard_map/all_to_all | solution.py:83
  107.0 1.2 copy.53
  108.2 29.5 %all-gather.6.cloned.1.call-done = bf16[96,96,128]{2,1,0:T(8,128)(2,1)} async-done(((bf16[12,96,128]{2,1,0:T(8,128)(2,1)}), bf16[96,96,128]{2,1,0:T(8,128)(2,1)}) %all-gather.6.cloned.1.call-update) | async-done | bytes 2359312 | tf_op jit(solution)/shard_map/all_gather | solution.py:88
  137.7 3.5 copy.52
  141.3 3.0 fusion.64
  144.2 1.6 copy.54
  145.8 0.3 bitcast_reduce_fusion
  146.2 0.7 multiply_reduce_fusion.5
  146.9 0.8 multiply_reduce_fusion.1
  147.7 1.5 add_convert_fusion.1
  149.4 1.2 copy.59
  150.6 1.2 copy.56
  151.8 0.5 multiply_convert_fusion.11
  152.3 0.5 fusion.9
  152.8 0.7 copy-done.12
  153.5 0.9 fusion.16
  154.4 1.3 fusion.17
  155.7 44.1 %all-gather.8.cloned.1.call-done = bf16[96,96,128]{2,1,0:T(8,128)(2,1)} async-done(((bf16[12,96,128]{2,1,0:T(8,128)(2,1)}), bf16[96,96,128]{2,1,0:T(8,128)(2,1)}) %all-gather.8.cloned.1.call-update) | async-done | bytes 2359312 | tf_op jit(solution)/shard_map/all_gather | solution.py:106
  199.8 3.5 copy.55
  203.3 3.8 %fusion.66 = f32[128,96,12]{1,2,0:T(8,128)} fusion(bf16[96,96,128]{1,0,2:T(8,128)(2,1)S(1)} %copy.55, bf16[12,96,128]{1,0,2:T(8,128)(2,1)} %copy.59), kind=kOutput, calls=%fused_computation.126 | convolution fusion | flops 28311552 | bytes 3244032 | tf_op jit(solution)/shard_map/kjc,ijc->kic/dot_general | solution.py:109
  207.1 2.4 copy.60
  209.4 2.9 fusion.65
  212.4 1.5 copy.57
  213.9 2.4 bitcast_multiply_fusion.3
  216.3 0.5 fusion.43
  216.8 0.5 copy-done.16
  217.3 1.0 fusion.13
  218.4 0.5 multiply_reduce_fusion.3
  218.9 0.8 multiply_reduce_fusion.2
  219.7 0.5 multiply_convert_fusion.12
  220.3 0.5 all-reduce.8.cloned.1.call-update
  220.8 1.5 fusion.19
  222.3 66.6 %all-reduce.10.cloned.1.call-done = (bf16[128,128]{1,0:T(8,128)(2,1)}, bf16[128,128]{1,0:T(8,128)(2,1)}, bf16[128]{0:T(256)(128)(2,1)}, bf16[128]{0:T(256)(128)(2,1)}) async-done(((bf16[128,128]{1,0:T(8,128)(2,1)}, bf16[128,128]{1,0:T(8,128)(2,1)}, bf16[128]{0:T(256)(128)(2,1)}, bf16[128]{0:T(256)(128)(2,1)}), (bf16[128,128]{1,0:T(8,128)(2,1)}, bf16[128,128]{1,0:T(8,128)(2,1)}, bf16[128]{0:T(256)(128)(2,1)}, ...) | async-done | bytes 66064 | tf_op jit(solution)/shard_map/psum | solution.py:119
  288.9 1.4 convert_element_type.109
  290.3 1.4 convert_element_type.111
  291.7 1.1 convert_element_type.113
  292.8 1.1 convert_element_type.115
  293.9 69.3 %all-reduce.8.cloned.1.call-done = bf16[128,512]{1,0:T(8,128)(2,1)} async-done(((bf16[128,512]{1,0:T(8,128)(2,1)}), bf16[128,512]{1,0:T(8,128)(2,1)}) %all-reduce.8.cloned.1.call-update) | async-done | bytes 131088 | tf_op jit(solution)/shard_map/psum | solution.py:118
  363.2 1.6 convert_element_type.107
  (71 shorter events, 1.4 us)
Async XLA Ops:
  7.2 73.9 %copy-start = (bf16[128,512]{1,0:T(8,128)(2,1)S(1)}, bf16[128,512]{1,0:T(8,128)(2,1)}, u32[]{:S(2)}) copy-start(bf16[128,512]{1,0:T(8,128)(2,1)} %param.26) | copy-start | bytes 393220
  7.2 64.5 %all-gather.4.cloned.1.call-start = ((), (), s32[]{:S(2)}) async-start(), calls=%async_computation.1 | async-start | bytes 2654208 | tf_op jit(solution)/shard_map/all_gather | solution.py:66
  15.9 2.4 copy-start.5
  15.9 2.4 copy-start.23
  15.9 2.4 copy-start.25
  17.0 120.7 %all-gather.6.cloned.1.call-start = ((), (), s32[]{:S(2)}) async-start(), calls=%async_computation.2 | async-start | bytes 2654208 | tf_op jit(solution)/shard_map/all_gather | solution.py:88
  75.2 3.1 copy-start.24
  78.0 1.0 copy-start.6
  78.0 1.2 copy-start.17
  78.0 1.2 copy-start.19
  78.1 2.6 copy-start.22
  79.8 0.8 copy-start.2
  81.1 7.4 %copy-start.14 = (bf16[12,96,128]{2,1,0:T(8,128)(2,1)}, bf16[12,96,128]{2,1,0:T(8,128)(2,1)S(1)}, u32[]{:S(2)}) copy-start(bf16[12,96,128]{2,1,0:T(8,128)(2,1)S(1)} %multiply_convert_fusion.4) | copy-start | bytes 884740
  81.5 1.4 copy-start.1
  82.9 5.5 %copy-start.20 = (bf16[128,128]{1,0:T(8,128)(2,1)S(1)}, bf16[128,128]{1,0:T(8,128)(2,1)}, u32[]{:S(2)}) copy-start(bf16[128,128]{1,0:T(8,128)(2,1)} %param.27) | copy-start | bytes 98308
  84.0 22.9 %copy-start.9 = (bf16[12,96,128]{2,1,0:T(8,128)(2,1)}, bf16[12,96,128]{2,1,0:T(8,128)(2,1)S(1)}, u32[]{:S(2)}) copy-start(bf16[12,96,128]{2,1,0:T(8,128)(2,1)S(1)} %get-tuple-element.22) | copy-start | bytes 884740
  84.9 22.0 %all-to-all-start = ((bf16[12,96,128]{2,0,1:T(8,128)(2,1)}), bf16[12,96,128]{2,0,1:T(8,128)(2,1)S(1)}, u32[]{:S(2)}, u32[]{:S(2)}) async-start(bf16[12,96,128]{2,0,1:T(8,128)(2,1)} %copy.49), calls=%async_computation | async-start | bytes 786432 | tf_op jit(solution)/shard_map/all_to_all | solution.py:83
  88.4 111.4 %all-gather.8.cloned.1.call-start = ((), (), s32[]{:S(2)}) async-start(), calls=%async_computation.3 | async-start | bytes 2654208 | tf_op jit(solution)/shard_map/all_gather | solution.py:106
  141.2 4.9 %copy-start.18 = (bf16[128,128]{1,0:T(8,128)(2,1)S(1)}, bf16[128,128]{1,0:T(8,128)(2,1)}, u32[]{:S(2)}) copy-start(bf16[128,128]{1,0:T(8,128)(2,1)} %param.29) | copy-start | bytes 98308
  141.2 4.9 %copy-start.21 = (f32[128]{0:T(128)S(1)}, f32[128]{0:T(128)}, u32[]{:S(2)}) copy-start(f32[128]{0:T(128)} %param.28) | copy-start | bytes 1540
  144.2 1.9 copy-start.4
  144.2 1.9 copy-start.7
  146.2 3.2 copy-start.11
  146.9 3.7 %copy-start.10 = (bf16[12,96,128]{2,1,0:T(8,128)(2,1)S(1)}, bf16[12,96,128]{2,1,0:T(8,128)(2,1)}, u32[]{:S(2)}) copy-start(bf16[12,96,128]{2,1,0:T(8,128)(2,1)} %copy-done.9) | copy-start | bytes 884740
  147.7 5.9 %copy-start.15 = (bf16[12,96,128]{2,1,0:T(8,128)(2,1)S(1)}, bf16[12,96,128]{2,1,0:T(8,128)(2,1)}, u32[]{:S(2)}) copy-start(bf16[12,96,128]{2,1,0:T(8,128)(2,1)} %copy-done.14) | copy-start | bytes 884740
  149.2 139.7 %all-reduce.10.cloned.1.call-start = ((), (), s32[]{:S(2)}) async-start(), calls=%async_computation.5 | async-start | bytes 133120 | tf_op jit(solution)/shard_map/psum | solution.py:119
  152.8 0.7 copy-start.12
  216.3 1.0 copy-start.16
  217.3 1.1 copy-start.3
  217.3 1.1 copy-start.13
  218.3 2.5 copy-start.8
  220.2 143.0 %all-reduce.8.cloned.1.call-start = ((), (), s32[]{:S(2)}) async-start(), calls=%async_computation.4 | async-start | bytes 262144 | tf_op jit(solution)/shard_map/psum | solution.py:118
Sparse Core Ops, SparseCore 0:
  17.1 54.5 all-gather.3
  84.1 53.5 all-gather.5
  149.3 50.4 all-gather.7
  220.3 68.4 all-reduce.9
  292.6 70.4 all-reduce.7
where the time goes:
time: 372 us; the launch traced here: 371 us
  waiting for transfers between devices  279 us (75%)
  local copies, waits for them, and re-layouts  27.9 us (8%)
  matrix products  23.6 us (6%)
  other arithmetic  22.7 us (6%)
  between operations  14.2 us (4%)
  starting transfers between devices  3.84 us (1%)
    psum x1, waiting for transfers between devices, shards(): lax.psum(grad_proj.astype(jnp.bfloat16), 'dap').astype(jnp.float32)  69.3 us
    psum x1, waiting for transfers between devices, shards(): lax.psum(grad_gate.astype(jnp.bfloat16), 'dap').astype(jnp.float32)  66.6 us
    all_gather x1, waiting for transfers between devices, shards(): lax.all_gather(right_b, 'dap', axis=0, tiled=True)  51.8 us
    all_gather x1, waiting for transfers between devices, shards(): shard_rows = lax.all_gather(grad_x_b, 'dap', axis=0, tiled=True)  44.1 us
    all_gather x1, waiting for transfers between devices, shards(): lax.all_gather(right_ib, 'dap', axis=0, tiled=True)  29.5 us
    all_to_all x1, waiting for transfers between devices, shards(): lax.all_to_all(left_ib, 'dap', split_axis=1, concat_axis=0, tiled=True)  17.3 us
  transfers between devices with their start and end apart: 6, of which 6 were waited for; matrix products, arithmetic and copies ran while one was open for 5% of the time, Pallas kernels for 0%

commit v1 on v0

--- a/solution.py
+++ b/solution.py
@@ -1,7 +1,18 @@
+import functools
 import jax
 import jax.numpy as jnp
 from jax import lax
 from jax.sharding import PartitionSpec as P
+
+
+def slots_find(work_x, axis_k, which_dim):
+    inter = lax.axis_size("dap")
+    step_out = jnp.stack(jnp.split(work_x, inter, axis_k), axis=0)
+    far_arr = lax.all_to_all(step_out, "dap", 0, 0)
+    return jnp.concatenate(far_arr, axis=which_dim)
+
+
+reach_the_target = functools.partial(slots_find, axis_k=1, which_dim=0)
 
 
 def layer_norm(values_in, gain):
@@ -80,7 +91,7 @@
     )
     left_ib = left_in.astype(bf16)
     right_ib = right_in.astype(bf16)
-    columns = lax.all_to_all(left_ib, "dap", split_axis=1, concat_axis=0, tiled=True)
+    columns = reach_the_target(left_ib)
     left_block = columns
     x_in = jnp.einsum(
         "kic,kjc->ijc",

time: 372 us -> 376 us (1.011)
  local copies, waits for them, and re-layouts: 27.9 us -> 32.3 us
    unnamed x52 -> x59, local copies, waits for them, and re-layouts: 3.78 us -> 8.27 us
  transfers between devices with their start and end apart: 6 -> 6, of which waited for: 6 -> 6; matrix products, arithmetic and copies ran while one was open for 5% -> 6% of each run, Pallas kernels for 0% -> 0%
where the time goes in v1:
time: 376 us; the launch traced here: 375 us
  waiting for transfers between devices  278 us (74%)
  local copies, waits for them, and re-layouts  32.3 us (9%)
  matrix products  23.7 us (6%)
  other arithmetic  22.6 us (6%)
  between operations  14.2 us (4%)
  starting transfers between devices  3.84 us (1%)
    psum x1, waiting for transfers between devices, shards(): lax.psum(grad_proj.astype(jnp.bfloat16), 'dap').astype(jnp.float32)  69.3 us
    psum x1, waiting for transfers between devices, shards(): lax.psum(grad_gate.astype(jnp.bfloat16), 'dap').astype(jnp.float32)  66.6 us
    all_gather x1, waiting for transfers between devices, shards(): lax.all_gather(right_b, 'dap', axis=0, tiled=True)  51.8 us
    all_gather x1, waiting for transfers between devices, shards(): shard_rows = lax.all_gather(grad_x_b, 'dap', axis=0, tiled=True)  43.9 us
    all_gather x1, waiting for transfers between devices, shards(): lax.all_gather(right_ib, 'dap', axis=0, tiled=True)  27.6 us
    all_to_all x1, waiting for transfers between devices, slots_find(): far_arr = lax.all_to_all(step_out, 'dap', 0, 0)  18.6 us
    unnamed x59, local copies, waits for them, and re-layouts  8.27 us
  transfers between devices with their start and end apart: 6, of which 6 were waited for; matrix products, arithmetic and copies ran while one was open for 6% of the time, Pallas kernels for 0%

profile of v1, /device:TPU:0, one launch (start us, length us, event | category | flops | bytes accessed | tf_op | source)
XLA Modules:
  0.0 375.1 jit_solution(12373985218139913331)
XLA Ops:
  7.2 0.7 dynamic_slice.7
  8.0 0.7 broadcast_compare_fusion
  8.7 0.8 slice_bitcast_fusion.9
  9.5 1.4 fusion.41
  10.9 1.6 multiply_reduce_fusion.7
  12.5 0.7 dynamic_slice.6
  13.2 0.7 multiply_convert_fusion.10
  13.9 1.9 fusion.47
  15.9 1.1 fusion.28
  17.0 1.2 copy.34
  18.3 1.7 fusion.8
  19.9 51.8 %all-gather.4.cloned.1.call-done = bf16[96,96,128]{2,1,0:T(8,128)(2,1)} async-done(((bf16[12,96,128]{2,1,0:T(8,128)(2,1)}), bf16[96,96,128]{2,1,0:T(8,128)(2,1)}) %all-gather.4.cloned.1.call-update) | async-done | bytes 2359312 | tf_op jit(solution)/shard_map/all_gather | solution.py:77
  71.7 3.5 copy.33
  75.2 2.8 fusion.70
  78.5 0.5 copy-done.6
  79.2 0.6 fusion.71
  81.5 1.4 copy-done.1
  83.0 1.1 multiply_convert_fusion.2
  84.0 0.7 fusion.58
  84.8 0.6 fusion.57
  85.4 0.6 fusion.56
  86.0 0.6 fusion.55
  86.6 0.6 fusion.54
  87.3 0.6 fusion.53
  87.9 0.6 fusion.52
  88.5 0.6 fusion.51
  89.1 3.5 all-to-all-start
  92.7 1.2 fusion.5
  93.8 18.6 %all-to-all-done = bf16[8,12,12,128]{3,2,1,0:T(8,128)(2,1)S(1)} async-done(((bf16[8,12,12,128]{3,2,1,0:T(8,128)(2,1)}), bf16[8,12,12,128]{3,2,1,0:T(8,128)(2,1)S(1)}, u32[]{:S(2)}, u32[]{:S(2)}) %all-to-all-start) | async-done | bytes 294944 | tf_op jit(solution)/shard_map/all_to_all | solution.py:11
  112.5 1.4 copy.37
  113.9 27.6 %all-gather.6.cloned.1.call-done = bf16[96,96,128]{2,1,0:T(8,128)(2,1)} async-done(((bf16[12,96,128]{2,1,0:T(8,128)(2,1)}), bf16[96,96,128]{2,1,0:T(8,128)(2,1)}) %all-gather.6.cloned.1.call-update) | async-done | bytes 2359312 | tf_op jit(solution)/shard_map/all_gather | solution.py:99
  141.5 3.5 copy.36
  145.1 3.0 fusion.72
  148.0 1.6 copy.38
  150.0 0.7 multiply_reduce_fusion.5
  150.7 0.8 multiply_reduce_fusion.1
  151.5 1.4 add_convert_fusion.1
  153.2 1.2 copy.43
  154.4 1.2 copy.40
  155.7 0.5 multiply_convert_fusion.11
  156.2 0.5 fusion.9
  156.7 0.7 copy-done.12
  157.4 0.9 fusion.16
  158.3 1.3 fusion.17
  159.6 43.9 %all-gather.8.cloned.1.call-done = bf16[96,96,128]{2,1,0:T(8,128)(2,1)} async-done(((bf16[12,96,128]{2,1,0:T(8,128)(2,1)}), bf16[96,96,128]{2,1,0:T(8,128)(2,1)}) %all-gather.8.cloned.1.call-update) | async-done | bytes 2359312 | tf_op jit(solution)/shard_map/all_gather | solution.py:117
  203.5 3.5 copy.39
  207.0 3.8 %fusion.74 = f32[128,96,12]{1,2,0:T(8,128)} fusion(bf16[96,96,128]{1,0,2:T(8,128)(2,1)S(1)} %copy.39, bf16[12,96,128]{1,0,2:T(8,128)(2,1)} %copy.43), kind=kOutput, calls=%fused_computation.142 | convolution fusion | flops 28311552 | bytes 3244032 | tf_op jit(solution)/shard_map/kjc,ijc->kic/dot_general | solution.py:120
  210.8 2.4 copy.44
  213.2 3.0 fusion.73
  216.1 1.5 copy.41
  217.7 2.4 bitcast_multiply_fusion.3
  221.0 1.0 fusion.13
  222.2 0.5 multiply_reduce_fusion.3
  222.7 0.8 multiply_reduce_fusion.2
  223.4 0.5 multiply_convert_fusion.12
  224.0 0.5 all-reduce.8.cloned.1.call-update
  224.6 1.5 fusion.19
  226.0 66.6 %all-reduce.10.cloned.1.call-done = (bf16[128,128]{1,0:T(8,128)(2,1)}, bf16[128,128]{1,0:T(8,128)(2,1)}, bf16[128]{0:T(256)(128)(2,1)}, bf16[128]{0:T(256)(128)(2,1)}) async-done(((bf16[128,128]{1,0:T(8,128)(2,1)}, bf16[128,128]{1,0:T(8,128)(2,1)}, bf16[128]{0:T(256)(128)(2,1)}, bf16[128]{0:T(256)(128)(2,1)}), (bf16[128,128]{1,0:T(8,128)(2,1)}, bf16[128,128]{1,0:T(8,128)(2,1)}, bf16[128]{0:T(256)(128)(2,1)}, ...) | async-done | bytes 66064 | tf_op jit(solution)/shard_map/psum | solution.py:130
  292.6 1.4 convert_element_type.109
  294.0 1.4 convert_element_type.111
  295.4 1.1 convert_element_type.113
  296.5 1.1 convert_element_type.115
  297.6 69.3 %all-reduce.8.cloned.1.call-done = bf16[128,512]{1,0:T(8,128)(2,1)} async-done(((bf16[128,512]{1,0:T(8,128)(2,1)}), bf16[128,512]{1,0:T(8,128)(2,1)}) %all-reduce.8.cloned.1.call-update) | async-done | bytes 131088 | tf_op jit(solution)/shard_map/psum | solution.py:129
  366.9 1.6 convert_element_type.107
  (76 shorter events, 4.2 us)
Async XLA Ops:
  7.2 73.9 %copy-start = (bf16[128,512]{1,0:T(8,128)(2,1)S(1)}, bf16[128,512]{1,0:T(8,128)(2,1)}, u32[]{:S(2)}) copy-start(bf16[128,512]{1,0:T(8,128)(2,1)} %param.26) | copy-start | bytes 393220
  7.2 64.5 %all-gather.4.cloned.1.call-start = ((), (), s32[]{:S(2)}) async-start(), calls=%async_computation.1 | async-start | bytes 2654208 | tf_op jit(solution)/shard_map/all_gather | solution.py:77
  15.9 2.4 copy-start.5
  15.9 2.4 copy-start.23
  15.9 2.4 copy-start.25
  17.0 124.5 %all-gather.6.cloned.1.call-start = ((), (), s32[]{:S(2)}) async-start(), calls=%async_computation.2 | async-start | bytes 2654208 | tf_op jit(solution)/shard_map/all_gather | solution.py:99
  75.2 3.1 copy-start.24
  78.0 1.0 copy-start.6
  78.0 1.2 copy-start.17
  78.0 1.2 copy-start.19
  78.1 2.6 copy-start.22
  79.8 0.8 copy-start.2
  81.1 11.6 %copy-start.14 = (bf16[12,96,128]{2,1,0:T(8,128)(2,1)}, bf16[12,96,128]{2,1,0:T(8,128)(2,1)S(1)}, u32[]{:S(2)}) copy-start(bf16[12,96,128]{2,1,0:T(8,128)(2,1)S(1)} %multiply_convert_fusion.4) | copy-start | bytes 884740
  81.5 1.4 copy-start.1
  82.9 9.7 %copy-start.20 = (bf16[128,128]{1,0:T(8,128)(2,1)S(1)}, bf16[128,128]{1,0:T(8,128)(2,1)}, u32[]{:S(2)}) copy-start(bf16[128,128]{1,0:T(8,128)(2,1)} %param.27) | copy-start | bytes 98308
  84.0 29.9 %copy-start.9 = (bf16[12,96,128]{2,1,0:T(8,128)(2,1)}, bf16[12,96,128]{2,1,0:T(8,128)(2,1)S(1)}, u32[]{:S(2)}) copy-start(bf16[12,96,128]{2,1,0:T(8,128)(2,1)S(1)} %get-tuple-element.22) | copy-start | bytes 884740
  89.1 23.3 %all-to-all-start = ((bf16[8,12,12,128]{3,2,1,0:T(8,128)(2,1)}), bf16[8,12,12,128]{3,2,1,0:T(8,128)(2,1)S(1)}, u32[]{:S(2)}, u32[]{:S(2)}) async-start(bf16[8,12,12,128]{3,2,1,0:T(8,128)(2,1)} %fusion.51), calls=%async_computation | async-start | bytes 786432 | tf_op jit(solution)/shard_map/all_to_all | solution.py:11
  92.6 110.9 %all-gather.8.cloned.1.call-start = ((), (), s32[]{:S(2)}) async-start(), calls=%async_computation.3 | async-start | bytes 2654208 | tf_op jit(solution)/shard_map/all_gather | solution.py:117
  145.0 4.9 %copy-start.18 = (bf16[128,128]{1,0:T(8,128)(2,1)S(1)}, bf16[128,128]{1,0:T(8,128)(2,1)}, u32[]{:S(2)}) copy-start(bf16[128,128]{1,0:T(8,128)(2,1)} %param.29) | copy-start | bytes 98308
  145.1 4.9 %copy-start.21 = (f32[128]{0:T(128)S(1)}, f32[128]{0:T(128)}, u32[]{:S(2)}) copy-start(f32[128]{0:T(128)} %param.28) | copy-start | bytes 1540
  148.0 1.9 copy-start.4
  148.0 1.9 copy-start.7
  150.0 3.2 copy-start.11
  150.7 3.7 copy-start.10
  151.5 5.9 %copy-start.15 = (bf16[12,96,128]{2,1,0:T(8,128)(2,1)S(1)}, bf16[12,96,128]{2,1,0:T(8,128)(2,1)}, u32[]{:S(2)}) copy-start(bf16[12,96,128]{2,1,0:T(8,128)(2,1)} %copy-done.14) | copy-start | bytes 884740
  153.0 139.7 %all-reduce.10.cloned.1.call-start = ((), (), s32[]{:S(2)}) async-start(), calls=%async_computation.5 | async-start | bytes 133120 | tf_op jit(solution)/shard_map/psum | solution.py:130
  156.7 0.7 copy-start.12
  220.0 1.0 copy-start.16
  221.0 1.1 copy-start.3
  221.0 1.1 copy-start.13
  222.1 2.5 copy-start.8
  224.0 143.0 %all-reduce.8.cloned.1.call-start = ((), (), s32[]{:S(2)}) async-start(), calls=%async_computation.4 | async-start | bytes 262144 | tf_op jit(solution)/shard_map/psum | solution.py:129
Sparse Core Ops, SparseCore 0:
  17.1 54.5 all-gather.3
  84.2 57.2 all-gather.5
  153.1 50.3 all-gather.7
  224.1 68.4 all-reduce.9
  296.4 70.4 all-reduce.7
